TPU v7x, 32 devices: a whole 2x2x4 slice. The times are simulated.
32 devices in a mesh: cp: 32 (over z, y, x, core).
Axes of the slice: x: 2, y: 2, z: 4, core: 2. Of those that a mesh axis runs over, the one named last changes fastest.
Arguments:
- queries: bfloat16 [4096, 16, 192], P('cp')
- latent: bfloat16 [4096, 512], P('cp')
- key_rope: bfloat16 [4096, 64], P('cp')
- w_uk: bfloat16 [512, 16, 128], replicated
- w_uv: bfloat16 [512, 16, 128], replicated
- d_out: bfloat16 [4096, 16, 128], P('cp')
Outputs:
- output 1: bfloat16 [4096, 16, 128], P('cp')
- output 2: bfloat16 [4096, 16, 192], P('cp')
- output 3: bfloat16 [4096, 512], P('cp')
- output 4: bfloat16 [4096, 64], P('cp')
- output 5: float32 [512, 16, 128], replicated
- output 6: float32 [512, 16, 128], replicated
All inputs are finite; a program needn't handle non-finite values.
Results may differ from a plain program's by a relative error of at most 0.02.
Values are sent between devices in bfloat16 or wider.
A program may use at most 1 GiB of HBM per device.

v0:
```python
import functools
import math

import jax
import jax.numpy as jnp
from jax import lax
from jax.experimental import pallas as pl
from jax.experimental.pallas import tpu as pltpu
from jax.sharding import PartitionSpec as P

MESH = pl.DeviceIdType.MESH
NX, NY = 2, 2
PLANE = NX * NY
BLK = 128
SUP = 256
CH = SUP * PLANE
NEG = -1e30
NT = (((1,), (1,)), ((), ()))
NN = (((1,), (0,)), ((), ()))
BF, F32 = jnp.bfloat16, jnp.float32


def mm(a, b, dims=NN):
    return lax.dot_general(a, b, dims, preferred_element_type=F32)


def pack_rope(x):
    return jnp.concatenate([x[:64], x[64:]], axis=1)


def kernel(nz, qk_dim, q_ref, do_raw, c_ref, rt_ref, wk_hbm, wv_hbm,
           o_hbm, dq_hbm, dc_hbm, dr_hbm, dwk_out, dwv_out,
           o_out, dq_out, dv_recv, dk_recv, o_fin, dc_fin, dr_fin, do_ref,
           w_big, w_stage, wt_cat, q_recv, do_recv, c_all, kr, v, kt, vt, s_buf, p_buf, p_store, ds_buf, dkr, dv,
           qt, dof, dot_, ot, dqt, lse, delta_s, o_send, dq_send, dv_msg, dv_part, dk_msg, dk_part,
           dwt, dw_msg, dw_part, dw_all,
           msg_ss, msg_rs, q_rs, do_rs, pair_s, pair_r, dw_sem, out_sem, w_sem,
           cg_rz, cg_rp, cg_ss, v_rz, v_rp, v_ss, k_rz, k_rp, k_ss):
    n_chip = PLANE * nz
    n_dev = 2 * n_chip
    n_sup = n_chip // 2
    me = lax.axis_index("cp")
    chip, par = me // 2, me % 2
    partner = 2 * chip + (1 - par)
    x, y, z = chip % NX, (chip // NX) % NY, chip // PLANE
    scale = 1.0 / math.sqrt(qk_dim)
    c1 = scale * math.log2(math.e)
    scope = jax.named_scope

    def chip_at(zq, yq, xq):
        return (zq * NY + yq) * NX + xq

    def col_chip(col, zq):
        return chip_at(zq, 1 - y if col >= 2 else y, 1 - x if col % 2 else x)

    def remote(src, dst, ssem, rsem, dev):
        return pltpu.make_async_remote_copy(src_ref=src, dst_ref=dst, send_sem=ssem, recv_sem=rsem,
                                            device_id=(dev,), device_id_type=MESH)

    def start(src, dst, ssem, rsem, dev):
        @pl.when(dev == me)
        def _():
            pltpu.make_async_copy(src, dst, rsem).start()

        @pl.when(dev != me)
        def _():
            remote(src, dst, ssem, rsem, dev).start()

    def arrived(dst, rsem):
        pltpu.make_async_copy(dst, dst, rsem).wait()

    def loop(lo, hi, f):
        def body(i, carry):
            f(i)
            return carry

        lax.fori_loop(lo, hi, body, 0)

    n_piece = 8

    def w_copy(i):
        src = wk_hbm if i < n_piece // 2 else wv_hbm
        return pltpu.make_async_copy(src.at[pl.ds(i % (n_piece // 2) * BLK, BLK)], w_stage.at[i % 2], w_sem.at[i % 2])

    for i in range(2):
        w_copy(i).start()

    def heads_first(x):
        return jnp.transpose(x, (1, 0, 2))

    with scope("barrier"):
        barrier = pltpu.get_barrier_semaphore()
        loop(1, n_dev, lambda i: pl.semaphore_signal(
            barrier, inc=1, device_id=(lax.rem(me + i, n_dev),), device_id_type=MESH))
        pl.semaphore_wait(barrier, n_dev - 1)

    class Gather:
        def __init__(self, buf, rows, split, rz, rp, ss, ready):
            self.buf, self.rows, self.split = buf, rows, split
            self.rz, self.rp, self.ss, self.ready = rz, rp, ss, ready
            self.dev_x = 2 * chip_at(z, y, 1 - x) + par
            self.dev_y = 2 * chip_at(z, 1 - y, x) + par

        def blk(self, col, zq):
            return self.buf.at[par, col_chip(col, zq)]

        def along_z(self, zq, to):
            b = self.blk(0, zq)
            return remote(b, b, self.ss.at[0], self.rz.at[0, zq], 2 * chip_at(to, y, x) + par)

        def to_x(self, col, zq):
            b = self.blk(col, zq)
            return remote(b, b, self.ss.at[0], self.rz.at[1, zq], self.dev_x)

        def to_y(self, col, zq):
            b = self.blk(col, zq)
            return remote(b, b, self.ss.at[0], self.rz.at[2, zq], self.dev_y)

        def part_y(self, col, zq):
            b = self.blk(col, zq).at[pl.ds(0, self.split)]
            return remote(b, b, self.ss.at[0], self.rz.at[3, zq], self.dev_y)

        def part_x(self, col, zq):
            b = self.blk(col, zq).at[pl.ds(self.split, self.rows - self.split)]
            return remote(b, b, self.ss.at[0], self.rz.at[3, zq], self.dev_x)

        def pair(self, col, zq):
            b = self.blk(col, zq)
            return remote(b, b, self.ss.at[1], self.rp.at[zq], partner)

        def own_col(self, zq):
            self.to_x(0, zq).start()
            self.to_y(0, zq).start()
            self.pair(0, zq).start()

        def xy(self, zq):
            self.to_x(1, zq).wait_recv()
            self.part_y(1, zq).start()
            self.pair(1, zq).start()
            self.to_y(2, zq).wait_recv()
            self.part_x(2, zq).start()
            self.pair(2, zq).start()

        def diag(self, zq):
            arrived(self.blk(3, zq), self.rz.at[3, zq])
            self.pair(3, zq).start()

        def pairs(self, zq):
            arrived(self.buf.at[1 - par, pl.ds(zq * PLANE, PLANE)], self.rp.at[zq])

        def begin(self):
            for d in range(1, nz):
                @pl.when(z + d < nz)
                def _():
                    self.along_z(z, z + d).start()

                @pl.when(z - d >= 0)
                def _():
                    self.along_z(z, z - d).start()

            self.own_col(z)

        def from_z(self, zq):
            self.along_z(zq, z).wait_recv()
            self.own_col(zq)

        def at(self, d, f):
            if d == 0:
                f(z)
                return

            @pl.when(z - d >= 0)
            def _():
                f(z - d)

            @pl.when(z + d < nz)
            def _():
                f(z + d)

        def last(self, zq):
            self.diag(zq)
            self.pairs(zq)
            self.ready(zq)

        def steps(self, tag, before_last):
            for d in range(1, nz):
                with scope(f"{tag}z{d}"):
                    self.at(d, self.from_z)
                with scope(f"{tag}xy{d - 1}"):
                    self.at(d - 1, self.xy)
                if d >= 2:
                    with scope(f"{tag}d{d - 2}"):
                        self.at(d - 2, self.last)
            with scope(f"{tag}xy{nz - 1}"):
                self.at(nz - 1, self.xy)
            for d in range(max(nz - 2, 0), nz):
                if d == nz - 1:
                    before_last()
                with scope(f"{tag}d{d}"):
                    self.at(d, self.last)

        def finish(self):
            arrived(self.buf.at[0, pl.ds(0, n_chip - 1)], self.ss.at[0])
            arrived(self.buf.at[0], self.ss.at[1])

    owner_core = lax.rem((chip + 1) // 2, 2)
    q_slot = 2 * (chip // 2) + par

    def sup_chip(s):
        return 2 * s + lax.rem(s + par, 2)

    def q_copy(i):
        head = lax.rem(chip + i, n_chip)
        return q_ref.at[head], q_recv.at[q_slot], msg_ss.at[0], q_rs.at[q_slot // 2], 2 * head + owner_core

    def do_copy(i):
        head = lax.rem(chip + i, n_chip)
        return do_ref.at[head], do_recv.at[q_slot], msg_ss.at[1], do_rs.at[q_slot // 2], 2 * head + owner_core

    def o_copy(s, i):
        return o_send.at[2 * s + i], o_out.at[chip], msg_ss.at[2], msg_rs.at[0], 2 * sup_chip(s) + i

    def dq_copy(s, i):
        return dq_send.at[2 * s + i], dq_out.at[chip], msg_ss.at[3], msg_rs.at[1], 2 * sup_chip(s) + i

    def dv_copy(ch):
        return dv_msg.at[par, ch], dv_recv.at[chip], msg_ss.at[4], msg_rs.at[2], 2 * ch + par

    def dk_copy(ch):
        return dk_msg.at[par, ch], dk_recv.at[chip], msg_ss.at[5], msg_rs.at[3], 2 * ch + par

    gc = Gather(c_all, 144, 80, cg_rz, cg_rp, cg_ss, None)
    with scope("send_c"):
        c_all[par, chip, pl.ds(0, BLK), :] = c_ref[...]
        for i in range(4):
            c_all[par, chip, pl.ds(BLK, 16), pl.ds(128 * i, 128)] = rt_ref[pl.ds(16 * i, 16), :]
        gc.begin()
    with scope("send_q"):
        def send_q(i):
            start(*q_copy(i))
            start(*do_copy(i))

        late = z >= nz // 2

        def lay_do(i):
            rows = pl.ds(pl.multiple_of(i * 32, 32), 32)
            do_ref[:, rows, :] = heads_first(do_raw[rows])

        loop(0, BLK // 32, lay_do)

        @pl.when(jnp.logical_not(late))
        def _():
            loop(0, n_chip, send_q)

    with scope("init"):
        dkr[...] = jnp.zeros_like(dkr)
        dv[...] = jnp.zeros_like(dv)
        for i in range(n_piece):
            w_copy(i).wait()

            def lay_w(r):
                w = heads_first(w_stage[i % 2, pl.ds(pl.multiple_of(r * 32, 32), 32)])
                rows = pl.ds(pl.multiple_of(i % (n_piece // 2) * BLK + r * 32, 32), 32)
                for h in range(n_chip):
                    w_big[rows, pl.ds(h * 256 + 128 * (i // (n_piece // 2)), 128)] = w[h]

            loop(0, BLK // 32, lay_w)
            if i + 2 < n_piece:
                w_copy(i + 2).start()
        wt_cat[...] = jnp.transpose(w_big[:, pl.ds(pl.multiple_of(chip * 256, 256), 256)].astype(F32)).astype(BF)
        qt[pl.ds(192, 64), :] = jnp.zeros((64, SUP), BF)

    def latent_of(ch):
        return jnp.concatenate([c_all[0, ch, pl.ds(0, BLK), :], c_all[1, ch, pl.ds(0, BLK), :]], axis=0)

    def up_project(ch):
        base = pl.multiple_of(ch * SUP, SUP)
        lat = latent_of(ch)
        kv = mm(lat, w_big[:, pl.ds(pl.multiple_of(chip * 256, 256), 256)]).astype(BF)
        kvt = mm(wt_cat[...], lat, NT).astype(BF)
        kr[pl.ds(base, SUP), pl.ds(0, 128)] = kv[:, :128]
        v[pl.ds(base, SUP), :] = kv[:, 128:]
        kt[pl.ds(0, 128), pl.ds(base, SUP)] = kvt[:128]
        vt[:, pl.ds(base, SUP)] = kvt[128:]
        for q in range(2):
            rt = jnp.concatenate([c_all[q, ch, pl.ds(BLK, 16), pl.ds(128 * i, 128)] for i in range(4)], axis=0)
            kt[pl.ds(128, 64), pl.ds(base + q * BLK, BLK)] = rt
            r = jnp.transpose(rt.astype(F32))
            kr[pl.ds(base + q * BLK, BLK), pl.ds(128, 128)] = jnp.concatenate(
                [r, jnp.zeros_like(r)], axis=1).astype(BF)

    diff = lax.broadcasted_iota(jnp.int32, (SUP, SUP), 0) - lax.broadcasted_iota(jnp.int32, (SUP, SUP), 1)

    def load_q(s):
        for i in range(2):
            qt[pl.ds(0, 192), pl.ds(i * BLK, BLK)] = q_recv[2 * s + i]
            dof[pl.ds(i * BLK, BLK), :] = do_recv[2 * s + i]

    def store_row(s):
        a = s // 2
        return (a + 1) * (a + s % 2) * CH

    def forward(s):
        ch = sup_chip(s)
        arrived(q_recv.at[pl.ds(2 * s, 2)], q_rs.at[s])
        arrived(do_recv.at[pl.ds(2 * s, 2)], do_rs.at[s])
        load_q(s)
        dot_[...] = jnp.transpose(dof[...].astype(F32))
        n_ch = s // 2 + 1

        def score(j, m8):
            for t in range(CH // SUP):
                r0 = pl.multiple_of(j * CH + t * SUP, SUP)
                st = mm(kr[pl.ds(r0, SUP), :], qt[...])
                st = jnp.where(diff <= ch * SUP - r0, st, NEG)
                s_buf[pl.ds(r0, SUP), :] = st
                m8 = jnp.maximum(m8, jnp.max(st.reshape(SUP // 8, 8, SUP), axis=0))
            return m8

        m8 = lax.fori_loop(0, n_ch, score, jnp.full((8, SUP), NEG, F32))
        m2 = jnp.max(m8, axis=0, keepdims=True) * c1
        ot[...] = jnp.zeros_like(ot)

        def values(j, l8):
            base = pl.multiple_of(j * CH, CH)
            for t in range(CH // SUP):
                p = jnp.exp2(s_buf[pl.ds(base + t * SUP, SUP), :] * c1 - m2)
                l8 = l8 + jnp.sum(p.reshape(SUP // 8, 8, SUP), axis=0)
                p_buf[pl.ds(t * SUP, SUP), :] = p.astype(BF)
            ot[...] += mm(vt[:, pl.ds(base, CH)], p_buf[...])
            return l8

        l8 = lax.fori_loop(0, n_ch, values, jnp.zeros((8, SUP), F32))
        l = jnp.sum(l8, axis=0, keepdims=True)
        o = ot[...] / l
        lse2 = m2 + jnp.log2(l)
        delta_s[s] = jnp.sum(o * dot_[...], axis=0, keepdims=True)
        o_rows = jnp.transpose(o)
        for i in range(2):
            o_send[2 * s + i] = o_rows[i * BLK:(i + 1) * BLK].astype(BF)
        for i in range(2):
            start(*o_copy(s, i))
        row0 = store_row(s)

        def values_grad(j):
            base = pl.multiple_of(j * CH, CH)
            for t in range(CH // SUP):
                rows = pl.ds(base + t * SUP, SUP)
                p = jnp.exp2(s_buf[rows, :] * c1 - lse2).astype(BF)
                p_store[pl.ds(pl.multiple_of(row0 + base + t * SUP, SUP), SUP), :] = p
                dv[rows, :] += mm(p, dof[...])

        loop(0, n_ch, values_grad)

    def backward(s):
        load_q(s)
        dqt[...] = jnp.zeros_like(dqt)
        row0 = store_row(s)
        delta = delta_s[s]

        def keys_grad(j):
            base = pl.multiple_of(j * CH, CH)
            for t in range(CH // SUP):
                rows = pl.ds(base + t * SUP, SUP)
                dp = mm(v[rows, :], dof[...], NT)
                p = p_store[pl.ds(pl.multiple_of(row0 + base + t * SUP, SUP), SUP), :].astype(F32)
                ds_buf[pl.ds(t * SUP, SUP), :] = (p * (dp - delta) * scale).astype(BF)
            for t in range(CH // SUP):
                rows = pl.ds(base + t * SUP, SUP)
                dkr[rows, :] += mm(ds_buf[pl.ds(t * SUP, SUP), :], qt[...], NT)
            dqt[...] += mm(kt[:, pl.ds(base, CH)], ds_buf[...])

        loop(0, s // 2 + 1, keys_grad)
        for i in range(2):
            dq_send[2 * s + i] = dqt[:, pl.ds(i * BLK, BLK)].astype(BF)
        for i in range(2):
            start(*dq_copy(s, i))

    def ready_c(zq):
        gc.pairs(zq)
        loop(zq * PLANE, (zq + 1) * PLANE, up_project)

    def col_ready(zq):
        @pl.when(z != zq)
        def _():
            gc.from_z(zq)

    def step_c(k):
        if k < nz:
            col_ready(k)
        if 0 <= k - 1 < nz:
            gc.xy(k - 1)
        if 0 <= k - 2 < nz:
            gc.diag(k - 2)
            ready_c(k - 2)

    for k in range(nz + 2):
        with scope(f"c{k}"):
            step_c(k)
            if k < 2:
                @pl.when(late)
                def _():
                    loop(k * n_chip // 2, (k + 1) * n_chip // 2, send_q)

        if k >= 2:
            with scope(f"fwd{k - 2}"):
                loop(2 * (k - 2), 2 * (k - 2) + 2, forward)

    def head_dw(k, lo, hi, grads):
        def add(ch):
            base = pl.multiple_of(ch * SUP, SUP)
            g = jnp.transpose(grads(pl.ds(base, SUP))).astype(BF)
            dwt[k] += mm(g, latent_of(ch))

        loop(lo, hi, add)

    def dw_exchange(k):
        dw_msg[k] = jnp.transpose(dwt[k]).reshape(2, SUP, 128)
        c = remote(dw_msg.at[k, 1 - par], dw_part.at[k], pair_s.at[k], pair_r.at[k], partner)
        c.start()
        return c

    def dw_begin(k, c):
        c.wait_recv()
        dw_all[k, par, chip] = dw_msg[k, par] + dw_part[k]

    def dw_out_copy(k, q, h):
        dst = dwk_out if k == 0 else dwv_out
        return pltpu.make_async_copy(dw_all.at[k, q, h], dst.at[pl.ds(q * SUP, SUP), h, 0], dw_sem.at[k])

    def put_dw(k):
        def put(zq):
            for q in range(2):
                loop(zq * PLANE, (zq + 1) * PLANE, lambda h: dw_out_copy(k, q, h).start())

        return put

    dwt[...] = jnp.zeros_like(dwt)
    gv = Gather(dw_all.at[1], SUP, 128, v_rz, v_rp, v_ss, put_dw(1))
    gk = Gather(dw_all.at[0], SUP, 128, k_rz, k_rp, k_ss, put_dw(0))
    with scope("dv"):
        def dv_out(ch):
            for q in range(2):
                dv_msg[q, ch] = dv[pl.ds(pl.multiple_of(ch * SUP, SUP) + q * BLK, BLK), :].astype(BF)

        loop(0, n_chip, dv_out)
        pair_dv = remote(dv_msg.at[1 - par], dv_part, pair_s.at[2], pair_r.at[2], partner)
        pair_dv.start()
        head_dw(1, 0, n_chip, lambda rows: dv[rows, :])
        pair_dwv = dw_exchange(1)
        pair_dv.wait_recv()

        def dv_add(ch):
            dv_msg[par, ch] = (dv_msg[par, ch].astype(F32) + dv_part[ch].astype(F32)).astype(BF)

        loop(0, n_chip, dv_add)
        dw_begin(1, pair_dwv)
        gv.begin()

        def dv_send(i):
            start(*dv_copy(lax.rem(chip + i, n_chip)))

        loop(0, n_chip, dv_send)

    pair_dk = [remote(dk_msg.at[1 - par, pl.ds(PLANE * g, PLANE)], dk_part.at[pl.ds(PLANE * g, PLANE)],
                      pair_s.at[3 + g], pair_r.at[3 + g], partner) for g in range(nz)]

    def dk_out(g):
        def put(ch):
            for q in range(2):
                rows = pl.ds(pl.multiple_of(ch * SUP, SUP) + q * BLK, BLK)
                dk_msg[q, ch, pl.ds(0, BLK), :] = dkr[rows, pl.ds(0, 128)].astype(BF)
                dk_msg[q, ch, pl.ds(BLK, 64), :] = pack_rope(dkr[rows, pl.ds(128, 128)][:, :64]).astype(BF)

        loop(PLANE * g, PLANE * (g + 1), put)
        pair_dk[g].start()
        head_dw(0, PLANE * g, PLANE * (g + 1), lambda rows: dkr[rows, pl.ds(0, 128)])

    def dk_add(g):
        pair_dk[g].wait_recv()

        def put(ch):
            dk_msg[par, ch] = (dk_msg[par, ch].astype(F32) + dk_part[ch].astype(F32)).astype(BF)

        loop(PLANE * g, PLANE * (g + 1), put)

    for g in reversed(range(nz)):
        for s in (2 * g + 1, 2 * g):
            with scope(f"bwd{s}"):
                backward(s)
        if g + 1 < nz:
            with scope(f"dks{g + 1}"):
                dk_add(g + 1)
        with scope(f"dko{g}"):
            dk_out(g)
        if g == 1:
            with scope("vz1"):
                gv.at(1, gv.from_z)

    with scope("dwk"):
        pair_dwk = dw_exchange(0)
        dw_begin(0, pair_dwk)
        gk.begin()
    with scope("dks0"):
        dk_add(0)
    with scope("vz"):
        for d in range(2, nz):
            gv.at(d, gv.from_z)
    with scope("vxy0"):
        gv.at(0, gv.xy)
    for d in range(nz):
        if d + 1 < nz:
            with scope(f"vxy{d + 1}"):
                gv.at(d + 1, gv.xy)
        with scope(f"vd{d}"):
            gv.at(d, gv.last)
            loop(d * n_chip // nz, (d + 1) * n_chip // nz, lambda i: start(*dk_copy(lax.rem(chip + i, n_chip))))
        if d == 0:
            with scope("ofin"):
                arrived(o_out, msg_rs.at[0])

                def lay_o(i):
                    rows = pl.ds(pl.multiple_of(i * 32, 32), 32)
                    o_fin[rows] = heads_first(o_out[:, rows, :])

                loop(0, BLK // 32, lay_o)

    def latent_grad():
        with scope("dc"):
            arrived(dv_recv, msg_rs.at[2])
            arrived(dk_recv, msg_rs.at[3])
            dkv = jnp.concatenate([g for h in range(n_chip) for g in (dk_recv[h, pl.ds(0, BLK), :], dv_recv[h])], axis=1)
            dc_fin[...] = mm(dkv, w_big[...], NT).astype(BF)
            dr = dk_recv[0, pl.ds(BLK, 64), :].astype(F32)
            for h in range(1, n_chip):
                dr = dr + dk_recv[h, pl.ds(BLK, 64), :].astype(F32)
            dr_fin[...] = jnp.transpose(jnp.concatenate([dr[:, :64], dr[:, 64:]], axis=0)).astype(BF)

    gk.steps("k", latent_grad)

    with scope("drain"):
        arrived(dq_out, msg_rs.at[1])
        outs = [pltpu.make_async_copy(buf, dst, out_sem.at[i]) for i, (buf, dst) in enumerate(
            ((dq_out, dq_hbm), (o_fin, o_hbm), (dc_fin, dc_hbm), (dr_fin, dr_hbm)))]
        for c in outs:
            c.start()
        for g in (gc, gv, gk):
            g.finish()
        for c in [pair_dv, pair_dwv, pair_dwk] + pair_dk:
            c.wait_send()
        for k, buf in enumerate((q_recv, do_recv, o_out, dq_out)):
            @pl.when(owner_core == par)
            def _():
                arrived(buf.at[pl.ds(0, n_chip - 1)], msg_ss.at[k])

            @pl.when(owner_core != par)
            def _():
                arrived(buf, msg_ss.at[k])
        for k, buf in enumerate((dv_recv, dk_recv)):
            arrived(buf.at[pl.ds(0, n_chip - 1)], msg_ss.at[4 + k])
        for k in range(2):
            arrived(dw_all.at[k], dw_sem.at[k])
        for c in outs:
            c.wait()


def copy_kernel(*refs):
    n = len(RESULT_PIECES)
    src, dst, buf, (sem_in, sem_out) = refs[:n], refs[n:2 * n], refs[2 * n:3 * n], refs[3 * n:]
    ins, outs = [], []
    for a, b, c, pieces in zip(src, dst, buf, RESULT_PIECES):
        size = a.shape[0] // pieces
        for i in range(pieces):
            rows = pl.ds(i * size, size)
            ins.append(pltpu.make_async_copy(a.at[rows], c.at[rows], sem_in.at[len(ins)]))
            outs.append(pltpu.make_async_copy(c.at[rows], b.at[rows], sem_out.at[len(outs)]))
    for c in ins:
        c.start()
    for c, d in zip(ins, outs):
        c.wait()
        d.start()
    for d in outs:
        d.wait()


RESULT_PIECES = (1, 1, 1, 1, 4, 4)


def copy_results(*arrays):
    hbm = pl.BlockSpec(memory_space=pl.ANY)
    shapes = tuple(jax.ShapeDtypeStruct(a.shape, a.dtype) for a in arrays)
    dma = pltpu.SemaphoreType.DMA((sum(RESULT_PIECES),))
    return pl.pallas_call(
        copy_kernel, out_shape=shapes, in_specs=[hbm] * len(arrays), out_specs=(hbm,) * len(arrays),
        scratch_shapes=[pltpu.VMEM(a.shape, a.dtype) for a in arrays] + [dma, dma],
    )(*arrays)


def solution(mesh):
    n_dev = mesh.shape["cp"]
    n_chip = n_dev // 2
    nz = n_chip // PLANE
    seq = n_dev * BLK
    seq_spec = P("cp")

    def local_step(queries, latent, key_rope, w_uk, w_uv, d_out):
        vm = pl.BlockSpec(memory_space=pltpu.VMEM)
        hbm = pl.BlockSpec(memory_space=pl.ANY)
        dma = pltpu.SemaphoreType.DMA
        gather_sems = [dma((4, nz)), dma((nz,)), dma((2,))]
        o, dq, dc, dr, dwk, dwv = pl.pallas_call(
            functools.partial(kernel, nz, queries.shape[-1]),
            out_shape=(jax.ShapeDtypeStruct((BLK, n_chip, 128), BF),
                       jax.ShapeDtypeStruct((n_chip, 192, BLK), BF),
                       jax.ShapeDtypeStruct((BLK, 512), BF),
                       jax.ShapeDtypeStruct((64, BLK), BF),
                       jax.ShapeDtypeStruct((512, n_chip, 1, 128), F32),
                       jax.ShapeDtypeStruct((512, n_chip, 1, 128), F32)),
            in_specs=[vm] * 4 + [hbm] * 2,
            out_specs=(hbm,) * 6,
            scratch_shapes=[
                pltpu.VMEM((n_chip, BLK, 128), BF),
                pltpu.VMEM((n_chip, 192, BLK), BF),
                pltpu.VMEM((n_chip, BLK, 128), BF),
                pltpu.VMEM((n_chip, 192, 128), BF),
                pltpu.VMEM((BLK, n_chip, 128), BF),
                pltpu.VMEM((BLK, 512), BF),
                pltpu.VMEM((64, BLK), BF),
                pltpu.VMEM((n_chip, BLK, 128), BF),
                pltpu.VMEM((512, n_chip * 256), BF),
                pltpu.VMEM((2, BLK, n_chip, 128), BF),
                pltpu.VMEM((256, 512), BF),
                pltpu.VMEM((n_chip, 192, BLK), BF),
                pltpu.VMEM((n_chip, BLK, 128), BF),
                pltpu.VMEM((2, n_chip, 144, 512), BF),
                pltpu.VMEM((seq, 256), BF),
                pltpu.VMEM((seq, 128), BF),
                pltpu.VMEM((192, seq), BF),
                pltpu.VMEM((128, seq), BF),
                pltpu.VMEM((seq, SUP), F32),
                pltpu.VMEM((CH, SUP), BF),
                pltpu.VMEM((nz * (nz + 1) * CH, SUP), BF),
                pltpu.VMEM((CH, SUP), BF),
                pltpu.VMEM((seq, 256), F32),
                pltpu.VMEM((seq, 128), F32),
                pltpu.VMEM((256, SUP), BF),
                pltpu.VMEM((SUP, 128), BF),
                pltpu.VMEM((128, SUP), F32),
                pltpu.VMEM((128, SUP), F32),
                pltpu.VMEM((192, SUP), F32),
                pltpu.VMEM((8, SUP), F32),
                pltpu.VMEM((n_chip // 2, 1, SUP), F32),
                pltpu.VMEM((n_chip, BLK, 128), BF),
                pltpu.VMEM((n_chip, 192, BLK), BF),
                pltpu.VMEM((2, n_chip, BLK, 128), BF),
                pltpu.VMEM((n_chip, BLK, 128), BF),
                pltpu.VMEM((2, n_chip, 192, 128), BF),
                pltpu.VMEM((n_chip, 192, 128), BF),
                pltpu.VMEM((2, 128, 512), F32),
                pltpu.VMEM((2, 2, SUP, 128), F32),
                pltpu.VMEM((2, SUP, 128), F32),
                pltpu.VMEM((2, 2, n_chip, SUP, 128), F32),
            ] + [dma((6,)), dma((4,)), dma((n_chip // 2,)), dma((n_chip // 2,))] + [dma((3 + nz,)), dma((3 + nz,)), dma((2,)), dma((4,)), dma((2,))] + gather_sems * 3,
            compiler_params=pltpu.CompilerParams(
                collective_id=0, has_side_effects=True, vmem_limit_bytes=62 * 1024 * 1024),
        )(queries.transpose(1, 2, 0), d_out, latent, key_rope.T, w_uk, w_uv)
        o, dq, dc, dr, dwk, dwv = copy_results(
            o, dq, dc, dr, dwk.reshape(512, n_chip, 128), dwv.reshape(512, n_chip, 128))
        return o, dq.transpose(2, 0, 1), dc, dr.T, dwk, dwv

    return jax.shard_map(local_step, mesh=mesh,
                         in_specs=(seq_spec, seq_spec, seq_spec, P(), P(), seq_spec),
                         out_specs=(seq_spec, seq_spec, seq_spec, seq_spec, P(), P()),
                         check_vma=False)
```

profile of v0, /device:TPU:17, one launch (start us, length us, event | category | flops | bytes accessed | tf_op | source)
XLA Modules:
  0.0 166.1 jit_solution(9398767661518334844)
XLA Ops:
  0.6 157.6 %shard_map.109 = (bf16[128,16,128]{2,1,0:T(8,128)(2,1)}, bf16[16,192,128]{2,1,0:T(8,128)(2,1)}, bf16[128,512]{1,0:T(8,128)(2,1)}, bf16[64,128]{1,0:T(8,128)(2,1)...) custom-call(bf16[16,192,128]{2,1,0:T(8,128)(2,1)} %bitcast.8, bf16[128,16,128]{2,1,0:T(8,128)(2,1)} %do_raw.1, ...), custom_call_target="tpu_custom_call" | custom-call | tf_op jit(solution)/shard_map/pallas_call | solution.py:611
  158.2 7.8 %shard_map.110 = (bf16[128,16,128]{2,1,0:T(8,128)(2,1)}, bf16[16,192,128]{2,1,0:T(8,128)(2,1)}, bf16[128,512]{1,0:T(8,128)(2,1)}, bf16[64,128]{1,0:T(8,128)(2,1)...) custom-call(bf16[128,16,128]{2,1,0:T(8,128)(2,1)} %get-tuple-element.18.refs_0_, ...), custom_call_target="tpu_custom_call" | custom-call | tf_op jit(solution)/shard_map/pallas_call | solution.py:593
where the time goes:
time: 166 us
  Pallas kernels  165 us (99%)
    pallas_call x1, Pallas kernels, local_step(): pl.pallas_call(functools.partial(kernel, nz, queries.shape[-1]), out_shap...  158 us
    pallas_call x1, Pallas kernels, copy_results(): pl.pallas_call(copy_kernel, out_shape=shapes, in_specs=[hbm] * len(arrays...  7.82 us

commit v1 on v0

--- a/solution.py
+++ b/solution.py
@@ -352,6 +352,10 @@
 
         loop(0, n_ch, values_grad)
 
+    def send_dq(s):
+        for i in range(2):
+            start(*dq_copy(s, i))
+
     def backward(s):
         load_q(s)
         dqt[...] = jnp.zeros_like(dqt)
@@ -373,8 +377,8 @@
         loop(0, s // 2 + 1, keys_grad)
         for i in range(2):
             dq_send[2 * s + i] = dqt[:, pl.ds(i * BLK, BLK)].astype(BF)
-        for i in range(2):
-            start(*dq_copy(s, i))
+        if s >= n_sup // 2:
+            send_dq(s)
 
     def ready_c(zq):
         gc.pairs(zq)
@@ -506,6 +510,8 @@
     with scope("vz"):
         for d in range(2, nz):
             gv.at(d, gv.from_z)
+        for s in reversed(range(n_sup // 2)):
+            send_dq(s)
     with scope("vxy0"):
         gv.at(0, gv.xy)
     for d in range(nz):

time: 166 us -> 166 us (level)
  no operation moved by 1% of the time
where the time goes in v1:
time: 166 us; the launch traced here: 165 us
  Pallas kernels  165 us (99%)
    pallas_call x1, Pallas kernels, local_step(): pl.pallas_call(functools.partial(kernel, nz, queries.shape[-1]), out_shap...  157 us
    pallas_call x1, Pallas kernels, copy_results(): pl.pallas_call(copy_kernel, out_shape=shapes, in_specs=[hbm] * len(arrays...  7.82 us

profile of v1, /device:TPU:17, one launch (start us, length us, event | category | flops | bytes accessed | tf_op | source)
XLA Modules:
  0.0 165.4 jit_solution(16063610781258406842)
XLA Ops:
  0.6 157.0 %shard_map.109 = (bf16[128,16,128]{2,1,0:T(8,128)(2,1)}, bf16[16,192,128]{2,1,0:T(8,128)(2,1)}, bf16[128,512]{1,0:T(8,128)(2,1)}, bf16[64,128]{1,0:T(8,128)(2,1)...) custom-call(bf16[16,192,128]{2,1,0:T(8,128)(2,1)} %bitcast.8, bf16[128,16,128]{2,1,0:T(8,128)(2,1)} %do_raw.1, ...), custom_call_target="tpu_custom_call" | custom-call | tf_op jit(solution)/shard_map/pallas_call | solution.py:617
  157.6 7.8 %shard_map.110 = (bf16[128,16,128]{2,1,0:T(8,128)(2,1)}, bf16[16,192,128]{2,1,0:T(8,128)(2,1)}, bf16[128,512]{1,0:T(8,128)(2,1)}, bf16[64,128]{1,0:T(8,128)(2,1)...) custom-call(bf16[128,16,128]{2,1,0:T(8,128)(2,1)} %get-tuple-element.18.refs_0_, ...), custom_call_target="tpu_custom_call" | custom-call | tf_op jit(solution)/shard_map/pallas_call | solution.py:599

commit v2 on v1

--- a/solution.py
+++ b/solution.py
@@ -497,8 +497,9 @@
                 dk_add(g + 1)
         with scope(f"dko{g}"):
             dk_out(g)
-        if g == 1:
+        if g == nz - 2:
             with scope("vz1"):
+                gv.at(0, gv.xy)
                 gv.at(1, gv.from_z)
 
     with scope("dwk"):
@@ -512,8 +513,6 @@
             gv.at(d, gv.from_z)
         for s in reversed(range(n_sup // 2)):
             send_dq(s)
-    with scope("vxy0"):
-        gv.at(0, gv.xy)
     for d in range(nz):
         if d + 1 < nz:
             with scope(f"vxy{d + 1}"):
@@ -589,7 +588,7 @@
         d.wait()
 
 
-RESULT_PIECES = (1, 1, 1, 1, 4, 4)
+RESULT_PIECES = (1, 2, 1, 1, 8, 8)
 
 
 def copy_results(*arrays):

time: 166 us -> 166 us (level)
  no operation moved by 1% of the time
where the time goes in v2:
time: 166 us
  Pallas kernels  165 us (99%)
    pallas_call x1, Pallas kernels, local_step(): pl.pallas_call(functools.partial(kernel, nz, queries.shape[-1]), out_shap...  157 us
    pallas_call x1, Pallas kernels, copy_results(): pl.pallas_call(copy_kernel, out_shape=shapes, in_specs=[hbm] * len(arrays...  7.84 us

profile of v2, /device:TPU:17, one launch (start us, length us, event | category | flops | bytes accessed | tf_op | source)
XLA Modules:
  0.0 165.6 jit_solution(10149123142811536316)
XLA Ops:
  0.6 157.1 %shard_map.109 = (bf16[128,16,128]{2,1,0:T(8,128)(2,1)}, bf16[16,192,128]{2,1,0:T(8,128)(2,1)}, bf16[128,512]{1,0:T(8,128)(2,1)}, bf16[64,128]{1,0:T(8,128)(2,1)...) custom-call(bf16[16,192,128]{2,1,0:T(8,128)(2,1)} %bitcast.8, bf16[128,16,128]{2,1,0:T(8,128)(2,1)} %do_raw.1, ...), custom_call_target="tpu_custom_call" | custom-call | tf_op jit(solution)/shard_map/pallas_call | solution.py:616
  157.8 7.8 %shard_map.110 = (bf16[128,16,128]{2,1,0:T(8,128)(2,1)}, bf16[16,192,128]{2,1,0:T(8,128)(2,1)}, bf16[128,512]{1,0:T(8,128)(2,1)}, bf16[64,128]{1,0:T(8,128)(2,1)...) custom-call(bf16[128,16,128]{2,1,0:T(8,128)(2,1)} %get-tuple-element.18.refs_0_, ...), custom_call_target="tpu_custom_call" | custom-call | tf_op jit(solution)/shard_map/pallas_call | solution.py:598

commit v3 on v2

--- a/solution.py
+++ b/solution.py
@@ -209,12 +209,16 @@
     def sup_chip(s):
         return 2 * s + lax.rem(s + par, 2)
 
+    def far_first(i):
+        half = n_chip // 2
+        return (1 - chip // half + i // half) % 2 * half + (chip + i) % half
+
     def q_copy(i):
-        head = lax.rem(chip + i, n_chip)
+        head = far_first(i)
         return q_ref.at[head], q_recv.at[q_slot], msg_ss.at[0], q_rs.at[q_slot // 2], 2 * head + owner_core
 
     def do_copy(i):
-        head = lax.rem(chip + i, n_chip)
+        head = far_first(i)
         return do_ref.at[head], do_recv.at[q_slot], msg_ss.at[1], do_rs.at[q_slot // 2], 2 * head + owner_core
 
     def o_copy(s, i):

time: 166 us -> 167 us (level)
  no operation moved by 1% of the time
where the time goes in v3:
time: 167 us
  Pallas kernels  166 us (99%)
    pallas_call x1, Pallas kernels, local_step(): pl.pallas_call(functools.partial(kernel, nz, queries.shape[-1]), out_shap...  158 us
    pallas_call x1, Pallas kernels, copy_results(): pl.pallas_call(copy_kernel, out_shape=shapes, in_specs=[hbm] * len(arrays...  7.84 us

profile of v3, /device:TPU:17, one launch (start us, length us, event | category | flops | bytes accessed | tf_op | source)
XLA Modules:
  0.0 166.9 jit_solution(14775056727049949557)
XLA Ops:
  0.6 158.5 %shard_map.109 = (bf16[128,16,128]{2,1,0:T(8,128)(2,1)}, bf16[16,192,128]{2,1,0:T(8,128)(2,1)}, bf16[128,512]{1,0:T(8,128)(2,1)}, bf16[64,128]{1,0:T(8,128)(2,1)...) custom-call(bf16[16,192,128]{2,1,0:T(8,128)(2,1)} %bitcast.8, bf16[128,16,128]{2,1,0:T(8,128)(2,1)} %do_raw.1, ...), custom_call_target="tpu_custom_call" | custom-call | tf_op jit(solution)/shard_map/pallas_call | solution.py:620
  159.1 7.8 %shard_map.110 = (bf16[128,16,128]{2,1,0:T(8,128)(2,1)}, bf16[16,192,128]{2,1,0:T(8,128)(2,1)}, bf16[128,512]{1,0:T(8,128)(2,1)}, bf16[64,128]{1,0:T(8,128)(2,1)...) custom-call(bf16[128,16,128]{2,1,0:T(8,128)(2,1)} %get-tuple-element.18.refs_0_, ...), custom_call_target="tpu_custom_call" | custom-call | tf_op jit(solution)/shard_map/pallas_call | solution.py:602

commit v4 on v1

--- a/solution.py
+++ b/solution.py
@@ -510,8 +510,6 @@
     with scope("vz"):
         for d in range(2, nz):
             gv.at(d, gv.from_z)
-        for s in reversed(range(n_sup // 2)):
-            send_dq(s)
     with scope("vxy0"):
         gv.at(0, gv.xy)
     for d in range(nz):
@@ -522,6 +520,8 @@
             gv.at(d, gv.last)
             loop(d * n_chip // nz, (d + 1) * n_chip // nz, lambda i: start(*dk_copy(lax.rem(chip + i, n_chip))))
         if d == 0:
+            for s in reversed(range(n_sup // 2)):
+                send_dq(s)
             with scope("ofin"):
                 arrived(o_out, msg_rs.at[0])
 

time: 166 us -> 166 us (level)
  no operation moved by 1% of the time
where the time goes in v4:
time: 166 us
  Pallas kernels  165 us (99%)
    pallas_call x1, Pallas kernels, local_step(): pl.pallas_call(functools.partial(kernel, nz, queries.shape[-1]), out_shap...  157 us
    pallas_call x1, Pallas kernels, copy_results(): pl.pallas_call(copy_kernel, out_shape=shapes, in_specs=[hbm] * len(arrays...  7.82 us

profile of v4, /device:TPU:17, one launch (start us, length us, event | category | flops | bytes accessed | tf_op | source)
XLA Modules:
  0.0 165.7 jit_solution(7274463283012763068)
XLA Ops:
  0.6 157.2 %shard_map.109 = (bf16[128,16,128]{2,1,0:T(8,128)(2,1)}, bf16[16,192,128]{2,1,0:T(8,128)(2,1)}, bf16[128,512]{1,0:T(8,128)(2,1)}, bf16[64,128]{1,0:T(8,128)(2,1)...) custom-call(bf16[16,192,128]{2,1,0:T(8,128)(2,1)} %bitcast.8, bf16[128,16,128]{2,1,0:T(8,128)(2,1)} %do_raw.1, ...), custom_call_target="tpu_custom_call" | custom-call | tf_op jit(solution)/shard_map/pallas_call | solution.py:617
  157.8 7.8 %shard_map.110 = (bf16[128,16,128]{2,1,0:T(8,128)(2,1)}, bf16[16,192,128]{2,1,0:T(8,128)(2,1)}, bf16[128,512]{1,0:T(8,128)(2,1)}, bf16[64,128]{1,0:T(8,128)(2,1)...) custom-call(bf16[128,16,128]{2,1,0:T(8,128)(2,1)} %get-tuple-element.18.refs_0_, ...), custom_call_target="tpu_custom_call" | custom-call | tf_op jit(solution)/shard_map/pallas_call | solution.py:599
